TPU v7x, 32 devices: a whole 2x2x4 slice. The times are simulated.
32 devices in a mesh: tm: 32 (over z, y, x, core), chan: 1.
Axes of the slice: x: 2, y: 2, z: 4, core: 2. Of those that a mesh axis runs over, the one named last changes fastest.
Arguments:
- signal: bfloat16 [3, 4096, 512], P(None, 'tm', 'chan'), may hold values from -6 to 6
- taps: float32 [10, 2, 512], P(None, None, 'chan'), may hold values from -3 to 3
- w_gate: bfloat16 [10, 512, 2, 512], P(None, None, None, 'chan'), may hold values from -0.25 to 0.25
- w_res: bfloat16 [10, 512, 512], P(None, None, 'chan'), may hold values from -0.25 to 0.25
- w_skip: bfloat16 [10, 512, 512], P(None, None, 'chan'), may hold values from -0.1875 to 0.1875
Outputs:
- stream: bfloat16 [3, 4096, 512], P(None, 'tm', 'chan')
- skips: bfloat16 [3, 4096, 512], P(None, 'tm', 'chan')
All inputs are finite; a program needn't handle non-finite values.
Results may differ from a plain program's by a relative error of at most 0.02.
Values may be sent and summed in bfloat16 or wider, within the bound.
A program may use at most 64 MiB of HBM per device.

v0:
```python
import functools

import jax
import jax.numpy as jnp
from jax import lax
from jax.experimental import pallas as pl
from jax.experimental.pallas import tpu as pltpu
from jax.sharding import PartitionSpec as P

MESH = pl.DeviceIdType.MESH
BF16, F32 = jnp.bfloat16, jnp.float32
ALIGN = 16
VMEM_LIMIT = 56000 * 1024


def shifted(value, axis, steps):
    count = lax.axis_size(axis)
    leading, last = (max(0, -steps), min(count, count - steps))
    return lax.ppermute(value, axis, [(source, source + steps) for source in range(leading, last)])


def delay_block(stream, delay, near_fn, far_fn):
    length = stream.shape[1]
    whole, rest = divmod(delay, length)
    if whole == 0:
        nearer = stream
    else:
        nearer = near_fn(stream, whole)
    if rest == 0:
        return nearer
    farther = far_fn(stream[:, length - rest :], whole + 1)
    return jnp.concatenate([farther, nearer[:, : length - rest]], axis=1)


def near_time(block, steps):
    return shifted(block, "tm", steps)


def far_time(block, steps):
    return shifted(block, "tm", steps)


def gate_units(hidden):
    return (jnp.tanh(hidden[:, :, 0]) * jax.nn.sigmoid(hidden[:, :, 1])).astype(jnp.bfloat16)


def local(signal, taps, w_gate, w_res, w_skip):
    stream = signal
    seqs, length, local_c = stream.shape
    skip = jnp.zeros((seqs, length, local_c), jnp.float32)
    for layer in range(taps.shape[0]):
        delayed = delay_block(stream, 2**layer, near_time, far_time)
        conv = (
            taps[layer, 0] * delayed.astype(jnp.float32)
            + taps[layer, 1] * stream.astype(jnp.float32)
        ).astype(jnp.bfloat16)
        gate_w = w_gate[layer]
        hidden = jnp.einsum(
            "stc,cko->stko",
            lax.all_gather(conv, "chan", axis=2, tiled=True),
            gate_w,
            preferred_element_type=jnp.float32,
        )
        gated = gate_units(hidden)
        res_w = w_res[layer]
        skip_w = w_skip[layer]
        piece = lax.all_gather(gated, "chan", axis=2, tiled=True)
        update = jnp.einsum("stc,co->sto", piece, res_w, preferred_element_type=jnp.float32)
        skip_part = jnp.einsum("stc,co->sto", piece, skip_w, preferred_element_type=jnp.float32)
        stream = (stream.astype(jnp.float32) + update).astype(jnp.bfloat16)
        skip = skip + skip_part
    return (stream, skip.astype(jnp.bfloat16))


def tanh_gate(filt, gate):
    return (jnp.tanh(filt) * (0.5 * jnp.tanh(0.5 * gate) + 0.5)).astype(BF16)


def split_pairs(pairs, out):
    width = pairs.shape[0]
    block = min(128, width)
    row = lax.broadcasted_iota(jnp.int32, (2 * block, 2 * block), 0)
    column = lax.broadcasted_iota(jnp.int32, (2 * block, 2 * block), 1)
    wanted = jnp.where(row < block, 2 * row, 2 * (row - block) + 1)
    order = jnp.where(column == wanted, 1.0, 0.0).astype(F32).astype(BF16)
    for at in range(0, width, block):
        both = pairs[at : at + block].reshape(2 * block, pairs.shape[2])
        sorted_rows = jnp.dot(order, both, preferred_element_type=F32).astype(BF16)
        out[0, at : at + block] = sorted_rows[:block]
        out[1, at : at + block] = sorted_rows[block:]


def kernel(n, layers, near, sig_hbm, taps_hbm, wg_hbm, wr_hbm, ws_hbm, out_x, out_skip, *scratch):
    sig, taps, raw, wg, wr, ws, xs, zs, skip, in_sem, w_sem, send_sem, recv_sem = scratch[:13]
    halos = scratch[13:]
    seqs, length, width = sig.shape
    me = lax.axis_index("tm")
    clean = near - 1
    held = zs.shape[0]
    steps = [max(1, 2**layer // length) for layer in range(layers)]
    reach = sorted(set(steps))
    rows_of = [min(length, max(ALIGN, 2**layer)) for layer in range(layers)]
    half = min(256, width)

    def weights(layer):
        return [
            pltpu.make_async_copy(wg_hbm.at[layer], raw.at[layer], w_sem.at[layer, 0]),
            pltpu.make_async_copy(wr_hbm.at[layer], wr.at[layer], w_sem.at[layer, 1]),
            pltpu.make_async_copy(ws_hbm.at[layer], ws.at[layer], w_sem.at[layer, 2]),
        ]

    inputs = [
        pltpu.make_async_copy(sig_hbm, sig, in_sem.at[0]),
        pltpu.make_async_copy(taps_hbm, taps, in_sem.at[1]),
    ]
    for copy in inputs:
        copy.start()
    for layer in range(layers):
        for copy in weights(layer):
            copy.start()

    barrier = pltpu.get_barrier_semaphore()
    for step in reach:
        for ok, other in ((me + step < n, me + step), (me >= step, me - step)):

            @pl.when(ok)
            def _(other=other):
                pl.semaphore_signal(barrier, inc=1, device_id={"tm": other}, device_id_type=MESH)

    def source(layer):
        return sig if layer == 0 else xs.at[layer - 1]

    def send(layer, s):
        rows = rows_of[layer]
        return pltpu.make_async_remote_copy(
            src_ref=source(layer).at[s, pl.ds(length - rows, rows)],
            dst_ref=halos[layer].at[s],
            send_sem=send_sem.at[layer, s],
            recv_sem=recv_sem.at[layer, s],
            device_id={"tm": me + steps[layer]},
            device_id_type=MESH,
        )

    def start_send(layer, which):
        @pl.when(me + steps[layer] < n)
        def _():
            for s in which:
                send(layer, s).start()

    def take(layer, which):
        @pl.when(me >= steps[layer])
        def _():
            for s in which:
                send(layer, s).wait_recv()

        @pl.when(me < steps[layer])
        def _():
            for s in which:
                halos[layer][s] = jnp.zeros(halos[layer].shape[1:], BF16)

    def load(layer, s, low, high):
        return source(layer)[s, low:high]

    def finish(layer, delayed, own, which, low, high):
        count = high - low
        own_f = jnp.concatenate(own, axis=0).astype(F32) if len(own) > 1 else own[0].astype(F32)
        late = jnp.concatenate(delayed, axis=0) if len(delayed) > 1 else delayed[0]
        conv = (taps[layer, 0:1] * late.astype(F32) + taps[layer, 1:2] * own_f).astype(BF16)
        parts = []
        for at in range(0, width, half):
            filt = jnp.dot(conv, wg[layer, 0, :, at : at + half], preferred_element_type=F32)
            gate = jnp.dot(conv, wg[layer, 1, :, at : at + half], preferred_element_type=F32)
            parts.append(tanh_gate(filt, gate))
        z = jnp.concatenate(parts, axis=1) if len(parts) > 1 else parts[0]
        last = layer == layers - 1
        if layer < held:
            for i, s in enumerate(which):
                zs[layer, s, low:high] = z[i * count : (i + 1) * count]
        for at in range(0, width, half):
            cols = slice(at, at + half)
            update = jnp.dot(z, wr[layer, :, cols], preferred_element_type=F32)
            new = (own_f[:, cols] + update).astype(BF16)
            for i, s in enumerate(which):
                part = new[i * count : (i + 1) * count]
                if last:
                    out_x[s, low:high, cols] = part
                else:
                    xs[layer, s, low:high, cols] = part
        if not last:
            yield
        if layer < held:
            return
        for at in range(0, width, half):
            cols = slice(at, at + half)
            more = jnp.dot(z, ws[layer, :, cols], preferred_element_type=F32)
            for i, s in enumerate(which):
                part = more[i * count : (i + 1) * count]
                part = skip[s, low:high, cols] + part
                if last:
                    out_skip[s, low:high, cols] = part.astype(BF16)
                else:
                    skip[s, low:high, cols] = part
        if last:
            yield

    every = list(range(seqs))
    top = [max(ALIGN, 2 ** (layer + 1)) for layer in range(clean)]
    first = [0 if 2 ** (layer + 2) <= ALIGN * 1 else 0 for layer in range(clean)]
    for layer in range(clean - 1, -1, -1):
        need = top[layer] if layer == clean - 1 else first[layer + 1] - 2 ** (layer + 1)
        first[layer] = max(0, min(need, top[layer]) // ALIGN * ALIGN)

    for copy in inputs:
        copy.wait()
    for layer in range(clean):
        delay, low = 2**layer, first[layer]
        for copy in weights(layer):
            copy.wait()
        split_pairs(raw.at[layer], wg.at[layer])
        delayed, own = [], []
        for s in every:
            if delay < ALIGN:
                begin = max(0, low - ALIGN)
                block = pltpu.roll(load(layer, s, begin, length).astype(F32), delay, 0)
                delayed.append(block[low - begin :])
            else:
                delayed.append(load(layer, s, low - delay, length - delay))
            own.append(load(layer, s, low, length))
        work = finish(layer, delayed, own, every, low, length)
        next(work)
        if layer == 0:
            total = sum(((me + step < n).astype(jnp.int32) + (me >= step).astype(jnp.int32)) for step in reach)
            pl.semaphore_wait(barrier, total)
            start_send(0, every)
        start_send(layer + 1, every)
        for _ in work:
            pass

    def arrive(layer):
        for copy in weights(layer):
            copy.wait()
        split_pairs(raw.at[layer], wg.at[layer])

    arrive(clean)

    for layer in range(clean):
        delay, high = 2**layer, top[layer]
        take(layer, every)
        delayed, own = [], []
        for s in every:
            rows = rows_of[layer]
            tail = halos[layer][s]
            if delay < ALIGN:
                joined = jnp.concatenate([tail.astype(F32), load(layer, s, 0, high).astype(F32)], axis=0)
                delayed.append(pltpu.roll(joined, delay, 0)[rows:])
            else:
                delayed.append(jnp.concatenate([tail, load(layer, s, 0, high - delay)], axis=0))
            own.append(load(layer, s, 0, high))
        for _ in finish(layer, delayed, own, every, 0, high):
            pass

    for layer in range(clean, layers):
        if layer == clean + 1:
            for later in range(layer, layers):
                arrive(later)
        for s in every:
            take(layer, [s])
            late = halos[layer][s]
            if 2**layer < length:
                late = jnp.concatenate([late, load(layer, s, 0, length - 2**layer)], axis=0)
            work = finish(layer, [late], [load(layer, s, 0, length)], [s], 0, length)
            next(work)
            if layer + 1 < layers:
                start_send(layer + 1, [s])
            for _ in work:
                pass
        if layer == held - 1:
            for at in range(0, width, half):
                total = None
                for before in range(held):
                    gated = zs[before].reshape(seqs * length, width)
                    more = jnp.dot(gated, ws[before, :, at : at + half], preferred_element_type=F32)
                    total = more if total is None else total + more
                skip[:, :, at : at + half] = total.reshape(seqs, length, half)

    for layer in range(layers):

        @pl.when(me + steps[layer] < n)
        def _(layer=layer):
            for s in every:
                send(layer, s).wait_send()


def fused(n, signal, taps, w_gate, w_res, w_skip):
    seqs, length, width = signal.shape
    layers = taps.shape[0]
    near = length.bit_length() - 1
    held = min(near + 1, layers - 1)
    halos = [
        pltpu.VMEM((seqs, min(length, max(ALIGN, 2**layer)), width), BF16) for layer in range(layers)
    ]
    flops = 2 * seqs * length * width * width * 4 * layers
    in_vmem, anywhere = pl.BlockSpec(memory_space=pltpu.VMEM), pl.BlockSpec(memory_space=pl.ANY)
    return pl.pallas_call(
        functools.partial(kernel, n, layers, near),
        out_shape=[pltpu.VMEM(signal.shape, BF16)] * 2,
        in_specs=[anywhere] * 5,
        out_specs=[in_vmem, in_vmem],
        scratch_shapes=[
            pltpu.VMEM(signal.shape, BF16),
            pltpu.VMEM(taps.shape, F32),
            pltpu.VMEM((layers, width, 2, width), BF16),
            pltpu.VMEM((layers, 2, width, width), BF16),
            pltpu.VMEM((layers, width, width), BF16),
            pltpu.VMEM((layers, width, width), BF16),
            pltpu.VMEM((layers - 1, seqs, length, width), BF16),
            pltpu.VMEM((held, seqs, length, width), BF16),
            pltpu.VMEM((seqs, length, width), F32),
            pltpu.SemaphoreType.DMA((2,)),
            pltpu.SemaphoreType.DMA((layers, 3)),
            pltpu.SemaphoreType.DMA((layers, seqs)),
            pltpu.SemaphoreType.DMA((layers, seqs)),
            *halos,
        ],
        compiler_params=pltpu.CompilerParams(collective_id=0, has_side_effects=True, vmem_limit_bytes=VMEM_LIMIT),
        cost_estimate=pl.CostEstimate(flops=flops, bytes_accessed=8 * layers * width * width, transcendentals=0),
        name="stack",
    )(signal, taps, w_gate, w_res, w_skip)


def solution(mesh):
    in_specs = (
        P(None, "tm", "chan"),
        P(None, None, "chan"),
        P(None, None, None, "chan"),
        P(None, None, "chan"),
        P(None, None, "chan"),
    )
    out_specs = (P(None, "tm", "chan"), P(None, "tm", "chan"))

    def body(*args):
        length, layers = args[0].shape[1], args[1].shape[0]
        power = length & (length - 1) == 0 and length >= 4 * ALIGN and 2 ** (layers - 1) >= length
        if mesh.shape["chan"] == 1 and power:
            return tuple(fused(mesh.shape["tm"], *args))
        return local(*args)

    return jax.shard_map(body, mesh=mesh, in_specs=in_specs, out_specs=out_specs, check_vma=False)
```

profile of v0, /device:TPU:24, one launch (start us, length us, event | category | flops | bytes accessed | tf_op | source)
XLA Modules:
  0.0 44.2 jit_solution(14474602183893549184)
XLA Ops:
  0.6 42.1 %stack.1 = (bf16[3,128,512]{2,1,0:T(8,128)(2,1)S(1)}, bf16[3,128,512]{2,1,0:T(8,128)(2,1)S(1)}) custom-call(bf16[3,128,512]{2,1,0:T(8,128)(2,1)} %sig_hbm.1, f32[10,2,512]{2,1,0:T(2,128)} %taps_hbm.1, bf16[10,512,2,512]{3,2,1,0:T(2,128)(2,1)} %wg_hbm.1, bf16[10,512,512]{2,1,0:T(8,128)(2,1)} %wr_hbm.1, bf16[10,512,512]{2,1,0:T(8,128)(2,1)} %ws_hbm.1), custom_call_target="tpu_custom_call" | custom-call | flops 8053063680 | bytes 20971520 | tf_op jit(solution)/shard_map/stack/pallas_call | solution.py:304
  42.7 0.7 %copy.9 = bf16[3,128,512]{2,1,0:T(8,128)(2,1)} copy(bf16[3,128,512]{2,1,0:T(8,128)(2,1)S(1)} %get-tuple-element.2) | data formatting | bytes 786432
  43.5 0.7 %copy.10 = bf16[3,128,512]{2,1,0:T(8,128)(2,1)} copy(bf16[3,128,512]{2,1,0:T(8,128)(2,1)S(1)} %get-tuple-element.3) | data formatting | bytes 786432
where the time goes:
time: 44.6 us; the launch traced here: 44.2 us
  Pallas kernels  42.1 us (94%)
  local copies, waits for them, and re-layouts  1.49 us (3%)
  between operations  0.64 us (1%)
    pallas_call x1, Pallas kernels, fused(): pl.pallas_call(functools.partial(kernel, n, layers, near), out_shape=[plt...  42.1 us
    unnamed x2, local copies, waits for them, and re-layouts  1.49 us

commit v1 on v0

v1 whole, which is shorter than its diff:
```python
import functools

import jax
import jax.numpy as jnp
from jax import lax
from jax.experimental import pallas as pl
from jax.experimental.pallas import tpu as pltpu
from jax.sharding import PartitionSpec as P

MESH = pl.DeviceIdType.MESH
BF16, F32 = jnp.bfloat16, jnp.float32
ALIGN = 16
VMEM_LIMIT = 56000 * 1024


def shifted(value, axis, steps):
    count = lax.axis_size(axis)
    leading, last = (max(0, -steps), min(count, count - steps))
    return lax.ppermute(value, axis, [(source, source + steps) for source in range(leading, last)])


def delay_block(stream, delay, near_fn, far_fn):
    length = stream.shape[1]
    whole, rest = divmod(delay, length)
    if whole == 0:
        nearer = stream
    else:
        nearer = near_fn(stream, whole)
    if rest == 0:
        return nearer
    farther = far_fn(stream[:, length - rest :], whole + 1)
    return jnp.concatenate([farther, nearer[:, : length - rest]], axis=1)


def near_time(block, steps):
    return shifted(block, "tm", steps)


def far_time(block, steps):
    return shifted(block, "tm", steps)


def gate_units(hidden):
    return (jnp.tanh(hidden[:, :, 0]) * jax.nn.sigmoid(hidden[:, :, 1])).astype(jnp.bfloat16)


def local(signal, taps, w_gate, w_res, w_skip):
    stream = signal
    seqs, length, local_c = stream.shape
    skip = jnp.zeros((seqs, length, local_c), jnp.float32)
    for layer in range(taps.shape[0]):
        delayed = delay_block(stream, 2**layer, near_time, far_time)
        conv = (
            taps[layer, 0] * delayed.astype(jnp.float32)
            + taps[layer, 1] * stream.astype(jnp.float32)
        ).astype(jnp.bfloat16)
        gate_w = w_gate[layer]
        hidden = jnp.einsum(
            "stc,cko->stko",
            lax.all_gather(conv, "chan", axis=2, tiled=True),
            gate_w,
            preferred_element_type=jnp.float32,
        )
        gated = gate_units(hidden)
        res_w = w_res[layer]
        skip_w = w_skip[layer]
        piece = lax.all_gather(gated, "chan", axis=2, tiled=True)
        update = jnp.einsum("stc,co->sto", piece, res_w, preferred_element_type=jnp.float32)
        skip_part = jnp.einsum("stc,co->sto", piece, skip_w, preferred_element_type=jnp.float32)
        stream = (stream.astype(jnp.float32) + update).astype(jnp.bfloat16)
        skip = skip + skip_part
    return (stream, skip.astype(jnp.bfloat16))


def tanh_gate(filt, gate):
    return (jnp.tanh(filt) * (0.5 * jnp.tanh(0.5 * gate) + 0.5)).astype(BF16)


def split_pairs(pairs, out):
    width = pairs.shape[0]
    block = min(128, width)
    row = lax.broadcasted_iota(jnp.int32, (2 * block, 2 * block), 0)
    column = lax.broadcasted_iota(jnp.int32, (2 * block, 2 * block), 1)
    wanted = jnp.where(row < block, 2 * row, 2 * (row - block) + 1)
    order = jnp.where(column == wanted, 1.0, 0.0).astype(F32).astype(BF16)
    for at in range(0, width, block):
        both = pairs[at : at + block].reshape(2 * block, pairs.shape[2])
        sorted_rows = jnp.dot(order, both, preferred_element_type=F32).astype(BF16)
        out[0, at : at + block] = sorted_rows[:block]
        out[1, at : at + block] = sorted_rows[block:]


P1, P2, P3, P4, P9 = range(5)
REACH = 4


def kernel(n, layers, near, sig_hbm, taps_hbm, wg_hbm, wr_hbm, ws_hbm, out_x, out_skip, *scratch):
    sig, taps, raw, wg, wr, ws, xs, zs, skip, ahead, far = scratch[:11]
    in_sem, w_sem, send_sem, recv_sem, far_send, far_recv = scratch[11:17]
    halos = scratch[17:]
    seqs, length, width = sig.shape
    me = lax.axis_index("tm")
    place = lax.rem(me, 4)
    core = lax.rem(me, 2)
    clean = near - 1
    rows_of = [max(ALIGN, 2**layer) for layer in range(near)]
    half = min(256, width)
    every = list(range(seqs))

    def weights(layer):
        return [
            pltpu.make_async_copy(wg_hbm.at[layer], raw.at[layer], w_sem.at[layer, 0]),
            pltpu.make_async_copy(wr_hbm.at[layer], wr.at[layer], w_sem.at[layer, 1]),
            pltpu.make_async_copy(ws_hbm.at[layer], ws.at[layer], w_sem.at[layer, 2]),
        ]

    inputs = [
        pltpu.make_async_copy(sig_hbm, sig, in_sem.at[0]),
        pltpu.make_async_copy(taps_hbm, taps, in_sem.at[1]),
    ]
    for copy in inputs:
        copy.start()
    for layer in range(layers):
        for copy in weights(layer):
            copy.start()

    barrier = pltpu.get_barrier_semaphore()
    for step in range(1, REACH + 1):
        for ok, other in ((me + step < n, me + step), (me >= step, me - step)):

            @pl.when(ok)
            def _(other=other):
                pl.semaphore_signal(barrier, inc=1, device_id={"tm": other}, device_id_type=MESH)

    def source(layer):
        return sig if layer == 0 else xs.at[layer - 1]

    def send(layer, s):
        rows = rows_of[layer]
        return pltpu.make_async_remote_copy(
            src_ref=source(layer).at[s, pl.ds(length - rows, rows)],
            dst_ref=halos[layer].at[s],
            send_sem=send_sem.at[layer, s],
            recv_sem=recv_sem.at[layer, s],
            device_id={"tm": me + 1},
            device_id_type=MESH,
        )

    def start_send(layer):
        @pl.when(me + 1 < n)
        def _():
            for s in every:
                send(layer, s).start()

    def take(layer):
        @pl.when(me >= 1)
        def _():
            for s in every:
                send(layer, s).wait_recv()

        @pl.when(me < 1)
        def _():
            for s in every:
                halos[layer][s] = jnp.zeros(halos[layer].shape[1:], BF16)

    def ship(slot, s, block, where, other):
        return pltpu.make_async_remote_copy(
            src_ref=block.at[s],
            dst_ref=far.at[where, s],
            send_sem=far_send.at[slot, s],
            recv_sem=far_recv.at[where, s],
            device_id={"tm": other},
            device_id_type=MESH,
        )

    last_near, last_far = xs.at[near - 1], xs.at[layers - 2]
    relay = (place == 3) & (me >= 7)
    routes = {
        "own": [
            ((place == 3) & (me + 4 < n), 0, last_near, P4, me + 4),
            ((place != 3) & (me + 2 < n), 0, last_near, P2, me + 2),
            ((place == 1) & (me + 3 < n), 1, last_near, P3, me + 3),
            (core == 0, 1, last_near, P1, me + 1),
        ],
        "relay": [
            (relay, 2, far.at[P4], P2, me - 2),
            (relay, 3, far.at[P4], P3, me - 1),
        ],
        "share": [
            ((core == 1) & (me >= 2), 4, far.at[P2], P1, me - 1),
            ((core == 0) & (me >= 2), 4, far.at[P2], P3, me + 1),
        ],
        "last": [(me + 4 < n, 5, last_far, P9, me + 4)],
    }

    def go(kind, s):
        for ok, slot, block, where, other in routes[kind]:

            @pl.when(ok)
            def _(slot=slot, block=block, where=where, other=other):
                ship(slot, s, block, where, other).start()

    def get(where, s, least):
        @pl.when(me >= least)
        def _():
            ship(0, s, last_near, where, me).wait_recv()

        @pl.when(me < least)
        def _():
            far[where, s] = jnp.zeros(far.shape[2:], BF16)

    def load(layer, s, low, high):
        return source(layer)[s, low:high]

    def stack(parts):
        return jnp.concatenate(parts, axis=0) if len(parts) > 1 else parts[0]

    def gated(layer, late, own_f):
        conv = (taps[layer, 0:1] * late.astype(F32) + taps[layer, 1:2] * own_f).astype(BF16)
        parts = []
        for at in range(0, width, half):
            filt = jnp.dot(conv, wg[layer, 0, :, at : at + half], preferred_element_type=F32)
            gate = jnp.dot(conv, wg[layer, 1, :, at : at + half], preferred_element_type=F32)
            parts.append(tanh_gate(filt, gate))
        return jnp.concatenate(parts, axis=1) if len(parts) > 1 else parts[0]

    def columns():
        return [slice(at, at + half) for at in range(0, width, half)]

    def renewed(layer, z, own_f, cols):
        return (own_f[:, cols] + jnp.dot(z, wr[layer, :, cols], preferred_element_type=F32)).astype(BF16)

    def finish(layer, delayed, own, which, low, high):
        count = high - low
        own_f = stack(own).astype(F32)
        z = gated(layer, stack(delayed), own_f)
        for i, s in enumerate(which):
            zs[layer, s, low:high] = z[i * count : (i + 1) * count]
        for cols in columns():
            new = renewed(layer, z, own_f, cols)
            for i, s in enumerate(which):
                xs[layer, s, low:high, cols] = new[i * count : (i + 1) * count]

    top = [max(ALIGN, 2 ** (layer + 1)) for layer in range(clean)]
    first = [0] * clean
    for layer in range(clean - 1, -1, -1):
        need = top[layer] if layer == clean - 1 else first[layer + 1] - 2 ** (layer + 1)
        first[layer] = max(0, min(need, top[layer]) // ALIGN * ALIGN)

    def arrive(layer):
        for copy in weights(layer):
            copy.wait()
        split_pairs(raw.at[layer], wg.at[layer])

    for copy in inputs:
        copy.wait()
    for layer in range(clean):
        delay, low = 2**layer, first[layer]
        arrive(layer)
        delayed, own = [], []
        for s in every:
            if delay < ALIGN:
                begin = max(0, low - ALIGN)
                block = pltpu.roll(load(layer, s, begin, length).astype(F32), delay, 0)
                delayed.append(block[low - begin :])
            else:
                delayed.append(load(layer, s, low - delay, length - delay))
            own.append(load(layer, s, low, length))
        finish(layer, delayed, own, every, low, length)
        if layer == 0:
            total = sum(
                ((me + step < n).astype(jnp.int32) + (me >= step).astype(jnp.int32)) for step in range(1, REACH + 1)
            )
            pl.semaphore_wait(barrier, total)
            start_send(0)
        start_send(layer + 1)

    arrive(clean)

    for layer in range(clean):
        delay, high = 2**layer, top[layer]
        take(layer)
        delayed, own = [], []
        for s in every:
            rows = rows_of[layer]
            tail = halos[layer][s]
            if delay < ALIGN:
                joined = jnp.concatenate([tail.astype(F32), load(layer, s, 0, high).astype(F32)], axis=0)
                delayed.append(pltpu.roll(joined, delay, 0)[rows:])
            else:
                delayed.append(jnp.concatenate([tail, load(layer, s, 0, high - delay)], axis=0))
            own.append(load(layer, s, 0, high))
        finish(layer, delayed, own, every, 0, high)

    take(clean)
    for s in every:
        late = jnp.concatenate([halos[clean][s], load(clean, s, 0, length - 2**clean)], axis=0)
        finish(clean, [late], [load(clean, s, 0, length)], [s], 0, length)
        go("own", s)

    for layer in range(near, layers):
        arrive(layer)

    def held_skip(span):
        for cols in columns():
            total = None
            for before in span:
                z = zs[before].reshape(seqs * length, width)
                more = jnp.dot(z, ws[before, :, cols], preferred_element_type=F32)
                total = more if total is None else total + more
            total = total.reshape(seqs, length, half)
            skip[:, :, cols] = total if span[0] == 0 else skip[:, :, cols] + total

    held_skip(range(near))

    for s in every:

        @pl.when(relay)
        def _(s=s):
            ship(0, s, last_near, P4, me).wait_recv()

        go("relay", s)
        get(P2, s, 2)
        go("share", s)
        get(P1, s, 1)
        get(P3, s, 3)
        late = jnp.concatenate([far[P1, s], far[P3, s]], axis=0)
        own_f = jnp.concatenate([xs[near - 1, s], far[P2, s]], axis=0).astype(F32)
        z = gated(near, late, own_f)
        zs[near, s] = z[:length]
        for cols in columns():
            new = renewed(near, z, own_f, cols)
            xs[near, s, :, cols] = new[:length]
            ahead[s, :, cols] = new[length:]
        own_f = xs[near, s].astype(F32)
        z = gated(near + 1, ahead[s], own_f)
        zs[near + 1, s] = z
        for cols in columns():
            xs[near + 1, s, :, cols] = renewed(near + 1, z, own_f, cols)
        go("last", s)

    held_skip(range(near, layers - 1))

    final = layers - 1
    for s in every:
        get(P9, s, 4)
        own_f = xs[final - 1, s].astype(F32)
        z = gated(final, far[P9, s], own_f)
        for cols in columns():
            out_x[s, :, cols] = renewed(final, z, own_f, cols)
        for cols in columns():
            more = jnp.dot(z, ws[final, :, cols], preferred_element_type=F32)
            out_skip[s, :, cols] = (skip[s, :, cols] + more).astype(BF16)

    @pl.when(me + 1 < n)
    def _():
        for layer in range(near):
            for s in every:
                send(layer, s).wait_send()

    for route in routes.values():
        for ok, slot, block, where, other in route:

            @pl.when(ok)
            def _(slot=slot, block=block, where=where, other=other):
                for s in every:
                    ship(slot, s, block, where, other).wait_send()


def fused(n, signal, taps, w_gate, w_res, w_skip):
    seqs, length, width = signal.shape
    layers = taps.shape[0]
    near = length.bit_length() - 1
    halos = [pltpu.VMEM((seqs, max(ALIGN, 2**layer), width), BF16) for layer in range(near)]
    flops = 2 * seqs * length * width * width * 4 * layers
    in_vmem, anywhere = pl.BlockSpec(memory_space=pltpu.VMEM), pl.BlockSpec(memory_space=pl.ANY)
    return pl.pallas_call(
        functools.partial(kernel, n, layers, near),
        out_shape=[pltpu.VMEM(signal.shape, BF16)] * 2,
        in_specs=[anywhere] * 5,
        out_specs=[in_vmem, in_vmem],
        scratch_shapes=[
            pltpu.VMEM(signal.shape, BF16),
            pltpu.VMEM(taps.shape, F32),
            pltpu.VMEM((layers, width, 2, width), BF16),
            pltpu.VMEM((layers, 2, width, width), BF16),
            pltpu.VMEM((layers, width, width), BF16),
            pltpu.VMEM((layers, width, width), BF16),
            pltpu.VMEM((layers - 1, seqs, length, width), BF16),
            pltpu.VMEM((layers - 1, seqs, length, width), BF16),
            pltpu.VMEM((seqs, length, width), F32),
            pltpu.VMEM((seqs, length, width), BF16),
            pltpu.VMEM((5, seqs, length, width), BF16),
            pltpu.SemaphoreType.DMA((2,)),
            pltpu.SemaphoreType.DMA((layers, 3)),
            pltpu.SemaphoreType.DMA((near, seqs)),
            pltpu.SemaphoreType.DMA((near, seqs)),
            pltpu.SemaphoreType.DMA((6, seqs)),
            pltpu.SemaphoreType.DMA((5, seqs)),
            *halos,
        ],
        compiler_params=pltpu.CompilerParams(collective_id=0, has_side_effects=True, vmem_limit_bytes=VMEM_LIMIT),
        cost_estimate=pl.CostEstimate(flops=flops, bytes_accessed=8 * layers * width * width, transcendentals=0),
        name="stack",
    )(signal, taps, w_gate, w_res, w_skip)


def solution(mesh):
    in_specs = (
        P(None, "tm", "chan"),
        P(None, None, "chan"),
        P(None, None, None, "chan"),
        P(None, None, "chan"),
        P(None, None, "chan"),
    )
    out_specs = (P(None, "tm", "chan"), P(None, "tm", "chan"))

    def body(*args):
        n, length, layers = mesh.shape["tm"], args[0].shape[1], args[1].shape[0]
        fits = length >= 4 * ALIGN and 2 ** (layers - 3) == length and n % 4 == 0
        if mesh.shape["chan"] == 1 and fits:
            return tuple(fused(n, *args))
        return local(*args)

    return jax.shard_map(body, mesh=mesh, in_specs=in_specs, out_specs=out_specs, check_vma=False)
```

time: 44.6 us -> 42 us (0.942)
  Pallas kernels: 42.1 us -> 39.4 us
    pallas_call x1, Pallas kernels: 42.1 us -> 39.4 us  [fused(): pl.pallas_call(functools.partial(kernel, n, layers, near), out_shape=[plt...]
where the time goes in v1:
time: 42 us; the launch traced here: 41.5 us
  Pallas kernels  39.4 us (94%)
  local copies, waits for them, and re-layouts  1.49 us (4%)
  between operations  0.64 us (2%)
    pallas_call x1, Pallas kernels, fused(): pl.pallas_call(functools.partial(kernel, n, layers, near), out_shape=[plt...  39.4 us
    unnamed x2, local copies, waits for them, and re-layouts  1.49 us

profile of v1, /device:TPU:24, one launch (start us, length us, event | category | flops | bytes accessed | tf_op | source)
XLA Modules:
  0.0 41.5 jit_solution(6844591449188814598)
XLA Ops:
  0.6 39.4 %stack.1 = (bf16[3,128,512]{2,1,0:T(8,128)(2,1)S(1)}, bf16[3,128,512]{2,1,0:T(8,128)(2,1)S(1)}) custom-call(bf16[3,128,512]{2,1,0:T(8,128)(2,1)} %sig_hbm.1, f32[10,2,512]{2,1,0:T(2,128)} %taps_hbm.1, bf16[10,512,2,512]{3,2,1,0:T(2,128)(2,1)} %wg_hbm.1, bf16[10,512,512]{2,1,0:T(8,128)(2,1)} %wr_hbm.1, bf16[10,512,512]{2,1,0:T(8,128)(2,1)} %ws_hbm.1), custom_call_target="tpu_custom_call" | custom-call | flops 8053063680 | bytes 20971520 | tf_op jit(solution)/shard_map/stack/pallas_call | solution.py:377
  40.0 0.7 %copy.9 = bf16[3,128,512]{2,1,0:T(8,128)(2,1)} copy(bf16[3,128,512]{2,1,0:T(8,128)(2,1)S(1)} %get-tuple-element.2) | data formatting | bytes 786432
  40.8 0.7 %copy.10 = bf16[3,128,512]{2,1,0:T(8,128)(2,1)} copy(bf16[3,128,512]{2,1,0:T(8,128)(2,1)S(1)} %get-tuple-element.3) | data formatting | bytes 786432

commit v2 on v1

--- a/solution.py
+++ b/solution.py
@@ -96,8 +96,8 @@
 
 def kernel(n, layers, near, sig_hbm, taps_hbm, wg_hbm, wr_hbm, ws_hbm, out_x, out_skip, *scratch):
     sig, taps, raw, wg, wr, ws, xs, zs, skip, ahead, far = scratch[:11]
-    in_sem, w_sem, send_sem, recv_sem, far_send, far_recv = scratch[11:17]
-    halos = scratch[17:]
+    in_sem, w_sem, send_sem, recv_sem, far_send, far_recv, order_sem = scratch[11:18]
+    halos = scratch[18:]
     seqs, length, width = sig.shape
     me = lax.axis_index("tm")
     place = lax.rem(me, 4)
@@ -107,6 +107,10 @@
     half = min(256, width)
     every = list(range(seqs))
 
+    def fence():
+        pl.semaphore_signal(order_sem, 1)
+        pl.semaphore_wait(order_sem, 1)
+
     def weights(layer):
         return [
             pltpu.make_async_copy(wg_hbm.at[layer], raw.at[layer], w_sem.at[layer, 0]),
@@ -120,6 +124,7 @@
     ]
     for copy in inputs:
         copy.start()
+    fence()
     for layer in range(layers):
         for copy in weights(layer):
             copy.start()
@@ -397,6 +402,7 @@
             pltpu.SemaphoreType.DMA((near, seqs)),
             pltpu.SemaphoreType.DMA((6, seqs)),
             pltpu.SemaphoreType.DMA((5, seqs)),
+            pltpu.SemaphoreType.REGULAR,
             *halos,
         ],
         compiler_params=pltpu.CompilerParams(collective_id=0, has_side_effects=True, vmem_limit_bytes=VMEM_LIMIT),

time: 42 us -> 36.9 us (0.88)
  Pallas kernels: 39.4 us -> 34.3 us
    pallas_call x1, Pallas kernels: 39.4 us -> 34.3 us  [fused(): pl.pallas_call(functools.partial(kernel, n, layers, near), out_shape=[plt...]
where the time goes in v2:
time: 36.9 us; the launch traced here: 36.4 us
  Pallas kernels  34.3 us (93%)
  local copies, waits for them, and re-layouts  1.49 us (4%)
  between operations  0.64 us (2%)
    pallas_call x1, Pallas kernels, fused(): pl.pallas_call(functools.partial(kernel, n, layers, near), out_shape=[plt...  34.3 us
    unnamed x2, local copies, waits for them, and re-layouts  1.49 us

profile of v2, /device:TPU:24, one launch (start us, length us, event | category | flops | bytes accessed | tf_op | source)
XLA Modules:
  0.0 36.4 jit_solution(12694697821457396927)
XLA Ops:
  0.6 34.3 %stack.1 = (bf16[3,128,512]{2,1,0:T(8,128)(2,1)S(1)}, bf16[3,128,512]{2,1,0:T(8,128)(2,1)S(1)}) custom-call(bf16[3,128,512]{2,1,0:T(8,128)(2,1)} %sig_hbm.1, f32[10,2,512]{2,1,0:T(2,128)} %taps_hbm.1, bf16[10,512,2,512]{3,2,1,0:T(2,128)(2,1)} %wg_hbm.1, bf16[10,512,512]{2,1,0:T(8,128)(2,1)} %wr_hbm.1, bf16[10,512,512]{2,1,0:T(8,128)(2,1)} %ws_hbm.1), custom_call_target="tpu_custom_call" | custom-call | flops 8053063680 | bytes 20971520 | tf_op jit(solution)/shard_map/stack/pallas_call | solution.py:382
  34.9 0.7 %copy.9 = bf16[3,128,512]{2,1,0:T(8,128)(2,1)} copy(bf16[3,128,512]{2,1,0:T(8,128)(2,1)S(1)} %get-tuple-element.2) | data formatting | bytes 786432
  35.7 0.7 %copy.10 = bf16[3,128,512]{2,1,0:T(8,128)(2,1)} copy(bf16[3,128,512]{2,1,0:T(8,128)(2,1)S(1)} %get-tuple-element.3) | data formatting | bytes 786432

commit v3 on v2

--- a/solution.py
+++ b/solution.py
@@ -76,14 +76,17 @@
     return (jnp.tanh(filt) * (0.5 * jnp.tanh(0.5 * gate) + 0.5)).astype(BF16)
 
 
-def split_pairs(pairs, out):
-    width = pairs.shape[0]
-    block = min(128, width)
+def pair_order(block):
     row = lax.broadcasted_iota(jnp.int32, (2 * block, 2 * block), 0)
     column = lax.broadcasted_iota(jnp.int32, (2 * block, 2 * block), 1)
     wanted = jnp.where(row < block, 2 * row, 2 * (row - block) + 1)
-    order = jnp.where(column == wanted, 1.0, 0.0).astype(F32).astype(BF16)
-    for at in range(0, width, block):
+    return jnp.where(column == wanted, 1.0, 0.0).astype(F32).astype(BF16)
+
+
+def split_pairs(pairs, out, order, blocks):
+    block = order.shape[0] // 2
+    for index in blocks:
+        at = index * block
         both = pairs[at : at + block].reshape(2 * block, pairs.shape[2])
         sorted_rows = jnp.dot(order, both, preferred_element_type=F32).astype(BF16)
         out[0, at : at + block] = sorted_rows[:block]
@@ -157,15 +160,15 @@
             for s in every:
                 send(layer, s).start()
 
-    def take(layer):
+    def take(layer, which):
         @pl.when(me >= 1)
         def _():
-            for s in every:
+            for s in which:
                 send(layer, s).wait_recv()
 
         @pl.when(me < 1)
         def _():
-            for s in every:
+            for s in which:
                 halos[layer][s] = jnp.zeros(halos[layer].shape[1:], BF16)
 
     def ship(slot, s, block, where, other):
@@ -235,12 +238,16 @@
     def renewed(layer, z, own_f, cols):
         return (own_f[:, cols] + jnp.dot(z, wr[layer, :, cols], preferred_element_type=F32)).astype(BF16)
 
-    def finish(layer, delayed, own, which, low, high):
+    def finish(layer, delayed, own, which, low, high, before=None, between=None):
         count = high - low
+        if before:
+            before()
         own_f = stack(own).astype(F32)
         z = gated(layer, stack(delayed), own_f)
         for i, s in enumerate(which):
             zs[layer, s, low:high] = z[i * count : (i + 1) * count]
+        if between:
+            between()
         for cols in columns():
             new = renewed(layer, z, own_f, cols)
             for i, s in enumerate(which):
@@ -252,16 +259,28 @@
         need = top[layer] if layer == clean - 1 else first[layer + 1] - 2 ** (layer + 1)
         first[layer] = max(0, min(need, top[layer]) // ALIGN * ALIGN)
 
-    def arrive(layer):
+    block = min(128, width)
+    order = pair_order(block)
+    blocks = list(range(width // block))
+
+    def landed(layer):
         for copy in weights(layer):
             copy.wait()
-        split_pairs(raw.at[layer], wg.at[layer])
+
+    def split(layer, which):
+        split_pairs(raw.at[layer], wg.at[layer], order, which)
+
+    def arrive(layer):
+        landed(layer)
+        split(layer, blocks)
 
     for copy in inputs:
         copy.wait()
+    arrive(0)
+    early, late_blocks = blocks[: len(blocks) // 2], blocks[len(blocks) // 2 :]
     for layer in range(clean):
         delay, low = 2**layer, first[layer]
-        arrive(layer)
+        landed(layer + 1)
         delayed, own = [], []
         for s in every:
             if delay < ALIGN:
@@ -271,7 +290,10 @@
             else:
                 delayed.append(load(layer, s, low - delay, length - delay))
             own.append(load(layer, s, low, length))
-        finish(layer, delayed, own, every, low, length)
+        finish(
+            layer, delayed, own, every, low, length,
+            lambda: split(layer + 1, early), lambda: split(layer + 1, late_blocks),
+        )
         if layer == 0:
             total = sum(
                 ((me + step < n).astype(jnp.int32) + (me >= step).astype(jnp.int32)) for step in range(1, REACH + 1)
@@ -280,11 +302,9 @@
             start_send(0)
         start_send(layer + 1)
 
-    arrive(clean)
-
     for layer in range(clean):
         delay, high = 2**layer, top[layer]
-        take(layer)
+        take(layer, every)
         delayed, own = [], []
         for s in every:
             rows = rows_of[layer]
@@ -297,8 +317,8 @@
             own.append(load(layer, s, 0, high))
         finish(layer, delayed, own, every, 0, high)
 
-    take(clean)
     for s in every:
+        take(clean, [s])
         late = jnp.concatenate([halos[clean][s], load(clean, s, 0, length - 2**clean)], axis=0)
         finish(clean, [late], [load(clean, s, 0, length)], [s], 0, length)
         go("own", s)
@@ -316,8 +336,6 @@
             total = total.reshape(seqs, length, half)
             skip[:, :, cols] = total if span[0] == 0 else skip[:, :, cols] + total
 
-    held_skip(range(near))
-
     for s in every:
 
         @pl.when(relay)
@@ -325,6 +343,10 @@
             ship(0, s, last_near, P4, me).wait_recv()
 
         go("relay", s)
+        if s < seqs - 1:
+            held_skip(range(near * s // (seqs - 1), near * (s + 1) // (seqs - 1)))
+
+    for s in every:
         get(P2, s, 2)
         go("share", s)
         get(P1, s, 1)

time: 36.9 us -> 36 us (0.976)
  the two profiles are of different devices: /device:TPU:24 before, /device:TPU:23 now
where the time goes in v3:
time: 36 us; the launch traced here: 35.8 us
  Pallas kernels  33.7 us (94%)
  local copies, waits for them, and re-layouts  1.49 us (4%)
  between operations  0.64 us (2%)
    pallas_call x1, Pallas kernels, fused(): pl.pallas_call(functools.partial(kernel, n, layers, near), out_shape=[plt...  33.7 us
    unnamed x2, local copies, waits for them, and re-layouts  1.49 us

profile of v3, /device:TPU:23, one launch (start us, length us, event | category | flops | bytes accessed | tf_op | source)
XLA Modules:
  0.0 35.8 jit_solution(4358418201597292385)
XLA Ops:
  0.6 33.7 %stack.1 = (bf16[3,128,512]{2,1,0:T(8,128)(2,1)S(1)}, bf16[3,128,512]{2,1,0:T(8,128)(2,1)S(1)}) custom-call(bf16[3,128,512]{2,1,0:T(8,128)(2,1)} %sig_hbm.1, f32[10,2,512]{2,1,0:T(2,128)} %taps_hbm.1, bf16[10,512,2,512]{3,2,1,0:T(2,128)(2,1)} %wg_hbm.1, bf16[10,512,512]{2,1,0:T(8,128)(2,1)} %wr_hbm.1, bf16[10,512,512]{2,1,0:T(8,128)(2,1)} %ws_hbm.1), custom_call_target="tpu_custom_call" | custom-call | flops 8053063680 | bytes 20971520 | tf_op jit(solution)/shard_map/stack/pallas_call | solution.py:404
  34.3 0.7 %copy.9 = bf16[3,128,512]{2,1,0:T(8,128)(2,1)} copy(bf16[3,128,512]{2,1,0:T(8,128)(2,1)S(1)} %get-tuple-element.2) | data formatting | bytes 786432
  35.1 0.7 %copy.10 = bf16[3,128,512]{2,1,0:T(8,128)(2,1)} copy(bf16[3,128,512]{2,1,0:T(8,128)(2,1)S(1)} %get-tuple-element.3) | data formatting | bytes 786432

commit v4 on v3

--- a/solution.py
+++ b/solution.py
@@ -125,12 +125,21 @@
         pltpu.make_async_copy(sig_hbm, sig, in_sem.at[0]),
         pltpu.make_async_copy(taps_hbm, taps, in_sem.at[1]),
     ]
+    weights(0)[0].start()
+    fence()
     for copy in inputs:
         copy.start()
     fence()
+    weights(0)[1].start()
+    fence()
+    for layer in range(1, layers):
+        for copy in weights(layer)[:2]:
+            copy.start()
+        if layer <= near:
+            fence()
+    fence()
     for layer in range(layers):
-        for copy in weights(layer):
-            copy.start()
+        weights(layer)[2].start()
 
     barrier = pltpu.get_barrier_semaphore()
     for step in range(1, REACH + 1):
@@ -195,9 +204,10 @@
             (relay, 3, far.at[P4], P3, me - 1),
         ],
         "share": [
-            ((core == 1) & (me >= 2), 4, far.at[P2], P1, me - 1),
+            ((place == 1) & (me >= 2), 4, far.at[P2], P1, me - 1),
             ((core == 0) & (me >= 2), 4, far.at[P2], P3, me + 1),
         ],
+        "early": [(place == 3, 4, far.at[P2], P1, me - 1)],
         "last": [(me + 4 < n, 5, last_far, P9, me + 4)],
     }
 
@@ -211,7 +221,7 @@
     def get(where, s, least):
         @pl.when(me >= least)
         def _():
-            ship(0, s, last_near, where, me).wait_recv()
+            ship(0, s, last_near, where, me - 1).wait_recv()
 
         @pl.when(me < least)
         def _():
@@ -264,7 +274,7 @@
     blocks = list(range(width // block))
 
     def landed(layer):
-        for copy in weights(layer):
+        for copy in weights(layer)[:2]:
             copy.wait()
 
     def split(layer, which):
@@ -274,9 +284,11 @@
         landed(layer)
         split(layer, blocks)
 
+    weights(0)[0].wait()
+    split(0, blocks)
     for copy in inputs:
         copy.wait()
-    arrive(0)
+    weights(0)[1].wait()
     early, late_blocks = blocks[: len(blocks) // 2], blocks[len(blocks) // 2 :]
     for layer in range(clean):
         delay, low = 2**layer, first[layer]
@@ -323,8 +335,28 @@
         finish(clean, [late], [load(clean, s, 0, length)], [s], 0, length)
         go("own", s)
 
-    for layer in range(near, layers):
-        arrive(layer)
+    def early(s):
+        @pl.when(place == 3)
+        def _():
+            ship(0, s, last_near, P2, me - 2).wait_recv()
+            ship(4, s, far.at[P2], P1, me - 1).start()
+
+        @pl.when(relay)
+        def _():
+            ship(0, s, last_near, P4, me - 2).wait_recv()
+
+        go("relay", s)
+
+    def share(s):
+        @pl.when((place != 3) & (me >= 2))
+        def _():
+            ship(0, s, last_near, P2, me - 2).wait_recv()
+
+        @pl.when(me < 2)
+        def _():
+            far[P2, s] = jnp.zeros(far.shape[2:], BF16)
+
+        go("share", s)
 
     def held_skip(span):
         for cols in columns():
@@ -336,19 +368,19 @@
             total = total.reshape(seqs, length, half)
             skip[:, :, cols] = total if span[0] == 0 else skip[:, :, cols] + total
 
+    arrive(near)
+    arrive(near + 1)
+    early(0)
+    for layer in range(near + 2, layers):
+        arrive(layer)
+    for layer in range(layers):
+        weights(layer)[2].wait()
+    held_skip(range(near))
+
     for s in every:
-
-        @pl.when(relay)
-        def _(s=s):
-            ship(0, s, last_near, P4, me).wait_recv()
-
-        go("relay", s)
-        if s < seqs - 1:
-            held_skip(range(near * s // (seqs - 1), near * (s + 1) // (seqs - 1)))
-
-    for s in every:
-        get(P2, s, 2)
-        go("share", s)
+        if s + 1 < seqs:
+            early(s + 1)
+        share(s)
         get(P1, s, 1)
         get(P3, s, 3)
         late = jnp.concatenate([far[P1, s], far[P3, s]], axis=0)

time: 36 us -> 35.2 us (0.978)
  the two profiles are of different devices: /device:TPU:23 before, /device:TPU:24 now
where the time goes in v4:
time: 35.2 us; the launch traced here: 34.8 us
  Pallas kernels  32.6 us (93%)
  local copies, waits for them, and re-layouts  1.49 us (4%)
  between operations  0.64 us (2%)
    pallas_call x1, Pallas kernels, fused(): pl.pallas_call(functools.partial(kernel, n, layers, near), out_shape=[plt...  32.6 us
    unnamed x2, local copies, waits for them, and re-layouts  1.49 us

profile of v4, /device:TPU:24, one launch (start us, length us, event | category | flops | bytes accessed | tf_op | source)
XLA Modules:
  0.0 34.8 jit_solution(14698129959537049940)
XLA Ops:
  0.6 32.6 %stack.1 = (bf16[3,128,512]{2,1,0:T(8,128)(2,1)S(1)}, bf16[3,128,512]{2,1,0:T(8,128)(2,1)S(1)}) custom-call(bf16[3,128,512]{2,1,0:T(8,128)(2,1)} %sig_hbm.1, f32[10,2,512]{2,1,0:T(2,128)} %taps_hbm.1, bf16[10,512,2,512]{3,2,1,0:T(2,128)(2,1)} %wg_hbm.1, bf16[10,512,512]{2,1,0:T(8,128)(2,1)} %wr_hbm.1, bf16[10,512,512]{2,1,0:T(8,128)(2,1)} %ws_hbm.1), custom_call_target="tpu_custom_call" | custom-call | flops 8053063680 | bytes 20971520 | tf_op jit(solution)/shard_map/stack/pallas_call | solution.py:436
  33.3 0.7 %copy.9 = bf16[3,128,512]{2,1,0:T(8,128)(2,1)} copy(bf16[3,128,512]{2,1,0:T(8,128)(2,1)S(1)} %get-tuple-element.2) | data formatting | bytes 786432
  34.0 0.7 %copy.10 = bf16[3,128,512]{2,1,0:T(8,128)(2,1)} copy(bf16[3,128,512]{2,1,0:T(8,128)(2,1)S(1)} %get-tuple-element.3) | data formatting | bytes 786432

commit v5 on v4

--- a/solution.py
+++ b/solution.py
@@ -95,6 +95,7 @@
 
 P1, P2, P3, P4, P9 = range(5)
 REACH = 4
+PARTS = 2
 
 
 def kernel(n, layers, near, sig_hbm, taps_hbm, wg_hbm, wr_hbm, ws_hbm, out_x, out_skip, *scratch):
@@ -180,12 +181,16 @@
             for s in which:
                 halos[layer][s] = jnp.zeros(halos[layer].shape[1:], BF16)
 
-    def ship(slot, s, block, where, other):
+    piece = length // PARTS
+    pieces = range(PARTS)
+
+    def ship(slot, s, u, block, where, other):
+        rows = pl.ds(u * piece, piece)
         return pltpu.make_async_remote_copy(
-            src_ref=block.at[s],
-            dst_ref=far.at[where, s],
-            send_sem=far_send.at[slot, s],
-            recv_sem=far_recv.at[where, s],
+            src_ref=block.at[s, rows],
+            dst_ref=far.at[where, s, rows],
+            send_sem=far_send.at[slot, s, u],
+            recv_sem=far_recv.at[where, s, u],
             device_id={"tm": other},
             device_id_type=MESH,
         )
@@ -211,17 +216,19 @@
         "last": [(me + 4 < n, 5, last_far, P9, me + 4)],
     }
 
-    def go(kind, s):
+    def go(kind, s, which=pieces):
         for ok, slot, block, where, other in routes[kind]:
 
             @pl.when(ok)
             def _(slot=slot, block=block, where=where, other=other):
-                ship(slot, s, block, where, other).start()
+                for u in which:
+                    ship(slot, s, u, block, where, other).start()
 
     def get(where, s, least):
         @pl.when(me >= least)
         def _():
-            ship(0, s, last_near, where, me - 1).wait_recv()
+            for u in pieces:
+                ship(0, s, u, last_near, where, me - 1).wait_recv()
 
         @pl.when(me < least)
         def _():
@@ -336,27 +343,33 @@
         go("own", s)
 
     def early(s):
-        @pl.when(place == 3)
-        def _():
-            ship(0, s, last_near, P2, me - 2).wait_recv()
-            ship(4, s, far.at[P2], P1, me - 1).start()
-
-        @pl.when(relay)
-        def _():
-            ship(0, s, last_near, P4, me - 2).wait_recv()
-
-        go("relay", s)
+        for u in pieces:
+
+            @pl.when(place == 3)
+            def _(u=u):
+                ship(0, s, u, last_near, P2, me - 2).wait_recv()
+                ship(4, s, u, far.at[P2], P1, me - 1).start()
+
+            @pl.when(relay)
+            def _(u=u):
+                ship(0, s, u, last_near, P4, me - 2).wait_recv()
+
+            go("relay", s, [u])
 
     def share(s):
-        @pl.when((place != 3) & (me >= 2))
-        def _():
-            ship(0, s, last_near, P2, me - 2).wait_recv()
-
-        @pl.when(me < 2)
-        def _():
-            far[P2, s] = jnp.zeros(far.shape[2:], BF16)
-
-        go("share", s)
+        for u in pieces:
+
+            @pl.when((place != 3) & (me >= 2))
+            def _(u=u):
+                ship(0, s, u, last_near, P2, me - 2).wait_recv()
+
+            if u == 0:
+
+                @pl.when(me < 2)
+                def _():
+                    far[P2, s] = jnp.zeros(far.shape[2:], BF16)
+
+            go("share", s, [u])
 
     def held_skip(span):
         for cols in columns():
@@ -375,10 +388,12 @@
         arrive(layer)
     for layer in range(layers):
         weights(layer)[2].wait()
-    held_skip(range(near))
+    held_skip(range(near // 2))
+    early(1)
+    held_skip(range(near // 2, near))
 
     for s in every:
-        if s + 1 < seqs:
+        if 1 < s + 1 < seqs:
             early(s + 1)
         share(s)
         get(P1, s, 1)
@@ -423,7 +438,8 @@
             @pl.when(ok)
             def _(slot=slot, block=block, where=where, other=other):
                 for s in every:
-                    ship(slot, s, block, where, other).wait_send()
+                    for u in pieces:
+                        ship(slot, s, u, block, where, other).wait_send()
 
 
 def fused(n, signal, taps, w_gate, w_res, w_skip):
@@ -454,8 +470,8 @@
             pltpu.SemaphoreType.DMA((layers, 3)),
             pltpu.SemaphoreType.DMA((near, seqs)),
             pltpu.SemaphoreType.DMA((near, seqs)),
-            pltpu.SemaphoreType.DMA((6, seqs)),
-            pltpu.SemaphoreType.DMA((5, seqs)),
+            pltpu.SemaphoreType.DMA((6, seqs, PARTS)),
+            pltpu.SemaphoreType.DMA((5, seqs, PARTS)),
             pltpu.SemaphoreType.REGULAR,
             *halos,
         ],

time: 35.2 us -> 34.9 us (level)
  no operation moved by 1% of the time
where the time goes in v5:
time: 34.9 us; the launch traced here: 34.8 us
  Pallas kernels  32.6 us (93%)
  local copies, waits for them, and re-layouts  1.49 us (4%)
  between operations  0.64 us (2%)
    pallas_call x1, Pallas kernels, fused(): pl.pallas_call(functools.partial(kernel, n, layers, near), out_shape=[plt...  32.6 us
    unnamed x2, local copies, waits for them, and re-layouts  1.49 us

profile of v5, /device:TPU:24, one launch (start us, length us, event | category | flops | bytes accessed | tf_op | source)
XLA Modules:
  0.0 34.8 jit_solution(3551435548816223766)
XLA Ops:
  0.6 32.6 %stack.1 = (bf16[3,128,512]{2,1,0:T(8,128)(2,1)S(1)}, bf16[3,128,512]{2,1,0:T(8,128)(2,1)S(1)}) custom-call(bf16[3,128,512]{2,1,0:T(8,128)(2,1)} %sig_hbm.1, f32[10,2,512]{2,1,0:T(2,128)} %taps_hbm.1, bf16[10,512,2,512]{3,2,1,0:T(2,128)(2,1)} %wg_hbm.1, bf16[10,512,512]{2,1,0:T(8,128)(2,1)} %wr_hbm.1, bf16[10,512,512]{2,1,0:T(8,128)(2,1)} %ws_hbm.1), custom_call_target="tpu_custom_call" | custom-call | flops 8053063680 | bytes 20971520 | tf_op jit(solution)/shard_map/stack/pallas_call | solution.py:452
  33.3 0.7 %copy.9 = bf16[3,128,512]{2,1,0:T(8,128)(2,1)} copy(bf16[3,128,512]{2,1,0:T(8,128)(2,1)S(1)} %get-tuple-element.2) | data formatting | bytes 786432
  34.0 0.7 %copy.10 = bf16[3,128,512]{2,1,0:T(8,128)(2,1)} copy(bf16[3,128,512]{2,1,0:T(8,128)(2,1)S(1)} %get-tuple-element.3) | data formatting | bytes 786432

commit v6 on v5

--- a/solution.py
+++ b/solution.py
@@ -200,9 +200,11 @@
     routes = {
         "own": [
             ((place == 3) & (me + 4 < n), 0, last_near, P4, me + 4),
+            (core == 0, 1, last_near, P1, me + 1),
+        ],
+        "next": [
             ((place != 3) & (me + 2 < n), 0, last_near, P2, me + 2),
             ((place == 1) & (me + 3 < n), 1, last_near, P3, me + 3),
-            (core == 0, 1, last_near, P1, me + 1),
         ],
         "relay": [
             (relay, 2, far.at[P4], P2, me - 2),
@@ -341,6 +343,8 @@
         late = jnp.concatenate([halos[clean][s], load(clean, s, 0, length - 2**clean)], axis=0)
         finish(clean, [late], [load(clean, s, 0, length)], [s], 0, length)
         go("own", s)
+        if s == 0:
+            go("next", s)
 
     def early(s):
         for u in pieces:
@@ -382,8 +386,12 @@
             skip[:, :, cols] = total if span[0] == 0 else skip[:, :, cols] + total
 
     arrive(near)
+    for s in every[1:2]:
+        go("next", s)
     arrive(near + 1)
     early(0)
+    for s in every[2:]:
+        go("next", s)
     for layer in range(near + 2, layers):
         arrive(layer)
     for layer in range(layers):

time: 34.9 us -> 34.9 us (level)
  no operation moved by 1% of the time
where the time goes in v6:
time: 34.9 us; the launch traced here: 34.8 us
  Pallas kernels  32.6 us (93%)
  local copies, waits for them, and re-layouts  1.49 us (4%)
  between operations  0.64 us (2%)
    pallas_call x1, Pallas kernels, fused(): pl.pallas_call(functools.partial(kernel, n, layers, near), out_shape=[plt...  32.6 us
    unnamed x2, local copies, waits for them, and re-layouts  1.49 us

profile of v6, /device:TPU:24, one launch (start us, length us, event | category | flops | bytes accessed | tf_op | source)
XLA Modules:
  0.0 34.8 jit_solution(8468874389678423689)
XLA Ops:
  0.6 32.6 %stack.1 = (bf16[3,128,512]{2,1,0:T(8,128)(2,1)S(1)}, bf16[3,128,512]{2,1,0:T(8,128)(2,1)S(1)}) custom-call(bf16[3,128,512]{2,1,0:T(8,128)(2,1)} %sig_hbm.1, f32[10,2,512]{2,1,0:T(2,128)} %taps_hbm.1, bf16[10,512,2,512]{3,2,1,0:T(2,128)(2,1)} %wg_hbm.1, bf16[10,512,512]{2,1,0:T(8,128)(2,1)} %wr_hbm.1, bf16[10,512,512]{2,1,0:T(8,128)(2,1)} %ws_hbm.1), custom_call_target="tpu_custom_call" | custom-call | flops 8053063680 | bytes 20971520 | tf_op jit(solution)/shard_map/stack/pallas_call | solution.py:460
  33.3 0.7 %copy.9 = bf16[3,128,512]{2,1,0:T(8,128)(2,1)} copy(bf16[3,128,512]{2,1,0:T(8,128)(2,1)S(1)} %get-tuple-element.2) | data formatting | bytes 786432
  34.0 0.7 %copy.10 = bf16[3,128,512]{2,1,0:T(8,128)(2,1)} copy(bf16[3,128,512]{2,1,0:T(8,128)(2,1)S(1)} %get-tuple-element.3) | data formatting | bytes 786432
